TPU v7x, 32 devices: a whole 2x2x4 slice. The times are simulated.
32 devices in a mesh: frame: 4 (over z), height: 4 (over y, x), dp: 2 (over core).
Axes of the slice: x: 2, y: 2, z: 4, core: 2. Of those that a mesh axis runs over, the one named last changes fastest.
Arguments:
- clip_latents: bfloat16 [2, 8, 64, 16, 320], P('dp', 'frame', 'height'), may hold values from -6 to 6
- out_grad: bfloat16 [2, 8, 64, 16, 320], P('dp', 'frame', 'height'), may hold values from -6 to 6
- box_mask: int32 [2, 8, 64, 16], P('dp', 'frame', 'height'), may hold values from 0 to 1, as said below
- attn_weights: bfloat16 [1280, 320], replicated, may hold values from -0.3125 to 0.3125
- conv_weights: bfloat16 [2880, 320], replicated, may hold values from -0.109375 to 0.109375
- time_bias: float32 [5, 8, 8], replicated, may hold values from -4 to 250
Outputs:
- grad_input: bfloat16 [2, 8, 64, 16, 320], P('dp', 'frame', 'height')
- grad_attn: float32 [1280, 320], P(('frame', 'height', 'dp'))
- grad_conv: float32 [2880, 320], P(('height', 'dp'))
Inputs may be any that keep to these rules, and one draw needn't show every extreme that they name: Each frame of each clip has one grounding box: box_mask is 1 on a rectangle of 16 to 32 rows and 4 to 8 columns, 0 elsewhere.
All inputs are finite; a program needn't handle non-finite values.
Results may differ from a plain program's by a relative error of at most 0.025.
Values may be sent and summed in bfloat16 or wider, within the bound.
No kernel may reach another device: no remote copies, remote signals or barrier semaphores. Data moves between devices by JAX's collectives and lax.ppermute only.
A program may use at most 64 MiB of HBM per device.

v0:
```python
import jax
import jax.numpy as jnp
from jax import lax
from jax.sharding import PartitionSpec as P

ground_bias = 2.0


def padded_2(block, sides, width):
    for axis, dim in sides:
        count = lax.axis_size(axis)
        forward = [(i, i + 1) for i in range(count - 1)]
        backward = [(target, source) for source, target in forward]
        low = lax.ppermute(
            lax.slice_in_dim(block, block.shape[dim] - width, None, axis=dim), axis, forward
        )
        high = lax.ppermute(lax.slice_in_dim(block, 0, width, axis=dim), axis, backward)
        block = jnp.concatenate([low, block, high], axis=dim)
    return block


def silu_slope(value):
    sig = jax.nn.sigmoid(value)
    return sig * (1.0 + value * (1.0 - sig))


def project(matrix, weight):
    flat_rows = matrix.reshape(-1, matrix.shape[-1])
    result = jnp.dot(flat_rows, weight, preferred_element_type=jnp.float32)
    return result.reshape(matrix.shape[:-1] + (weight.shape[1],))


def project_back(matrix, weight):
    flat_rows = matrix.reshape(-1, matrix.shape[-1])
    result = lax.dot_general(
        flat_rows, weight, (((1,), (1,)), ((), ())), preferred_element_type=jnp.float32
    )
    return result.reshape(matrix.shape[:-1] + (weight.shape[0],))


def cross(left, right):
    left_rows = left.reshape(-1, left.shape[-1])
    right_rows = right.reshape(-1, right.shape[-1])
    return lax.dot_general(
        left_rows, right_rows, (((0,), (0,)), ((), ())), preferred_element_type=jnp.float32
    )


def body(clip_latents, out_grad, box_mask, attn_weights, conv_weights, time_bias):
    clip_count, frame_count, row_count, col_count, channels = clip_latents.shape
    head_count = time_bias.shape[0]
    all_frames = time_bias.shape[1]
    head_size = channels // head_count
    pixels = row_count * col_count
    scaling = head_size ** (-0.5)
    w_query = attn_weights[:channels]
    w_key = attn_weights[channels : 2 * channels]
    w_value = attn_weights[2 * channels : 3 * channels]
    w_out = attn_weights[3 * channels :]
    flat_x = clip_latents.reshape(clip_count, frame_count, pixels, channels)
    flat_marks = box_mask.reshape(clip_count, frame_count, pixels).astype(jnp.bfloat16)
    latents_t, marks_t = (
        lax.all_to_all(flat_x, "frame", split_axis=2, concat_axis=1, tiled=True),
        lax.all_to_all(flat_marks, "frame", split_axis=2, concat_axis=1, tiled=True),
    )
    query_t = project(latents_t, w_query).astype(jnp.bfloat16)
    key_t = project(latents_t, w_key).astype(jnp.bfloat16)
    value_t = project(latents_t, w_value).astype(jnp.bfloat16)
    column_tokens = query_t.shape[2]
    head_shape = (clip_count, all_frames, column_tokens, head_count, head_size)
    qh = query_t.reshape(head_shape)
    kh = key_t.reshape(head_shape)
    vh = value_t.reshape(head_shape)
    mark_bias = ground_bias * jnp.transpose(marks_t.astype(jnp.float32), (0, 2, 1))
    score_bias = time_bias[None, None] + mark_bias[:, :, None, None, :]
    scores = (
        jnp.einsum("ctnhd,cunhd->cnhtu", qh, kh, preferred_element_type=jnp.float32) * scaling
        + score_bias
    )
    prob_full = jax.nn.softmax(scores, axis=-1)
    prob_half = prob_full.astype(jnp.bfloat16)
    mixed_t = jnp.einsum(
        "cnhtu,cunhd->ctnhd", prob_half, vh, preferred_element_type=jnp.float32
    ).astype(jnp.bfloat16)
    mixed_t = mixed_t.reshape(clip_count, all_frames, column_tokens, channels)
    mixed_rows = lax.all_to_all(mixed_t, "frame", split_axis=1, concat_axis=2, tiled=True)
    residual = (flat_x.astype(jnp.float32) + project(mixed_rows, w_out)).astype(jnp.bfloat16)
    activated = jax.nn.silu(residual.astype(jnp.float32)).astype(jnp.bfloat16)
    out_flat = out_grad.reshape(clip_count, frame_count, pixels, channels)
    stacked = jnp.concatenate([activated, out_flat], axis=-1).reshape(
        clip_count, frame_count, row_count, col_count, 2 * channels
    )
    padded = padded_2(stacked, (("height", 2),), 1)
    padded = jnp.pad(padded, ((0, 0), (0, 0), (0, 0), (1, 1), (0, 0)))
    act_pad = padded[..., :channels]
    grad_pad = padded[..., channels:]
    out_rows = out_grad.reshape(-1, channels)
    delta_sum = jnp.zeros((out_rows.shape[0], channels), jnp.float32)
    conv_terms = []
    for row_step in (-1, 0, 1):
        for col_step in (-1, 0, 1):
            tap_index = 3 * (row_step + 1) + col_step + 1
            tap_weight = conv_weights[tap_index * channels : (tap_index + 1) * channels]
            shifted = grad_pad[
                :,
                :,
                1 - row_step : 1 - row_step + row_count,
                1 - col_step : 1 - col_step + col_count,
                :,
            ]
            delta_sum = delta_sum + project_back(shifted.reshape(-1, channels), tap_weight)
            moved_rows = act_pad[
                :,
                :,
                1 + row_step : 1 + row_step + row_count,
                1 + col_step : 1 + col_step + col_count,
                :,
            ]
            conv_terms.append(cross(moved_rows, out_rows))
    residual_flat = residual.reshape(-1, channels).astype(jnp.float32)
    upstream = (out_rows.astype(jnp.float32) + silu_slope(residual_flat) * delta_sum).astype(
        jnp.bfloat16
    )
    d_mixed = (
        project_back(upstream, w_out)
        .astype(jnp.bfloat16)
        .reshape(clip_count, frame_count, pixels, channels)
    )
    d_mixed_t = lax.all_to_all(d_mixed, "frame", split_axis=2, concat_axis=1, tiled=True)
    dh = d_mixed_t.reshape(head_shape)
    d_prob = jnp.einsum("ctnhd,cunhd->cnhtu", dh, vh, preferred_element_type=jnp.float32)
    row_dot = jnp.sum(prob_full * d_prob, axis=-1, keepdims=True)
    d_scores = (prob_full * (d_prob - row_dot)).astype(jnp.bfloat16)
    column_shape = (clip_count, all_frames, column_tokens, channels)
    d_query = (
        (
            jnp.einsum("cnhtu,cunhd->ctnhd", d_scores, kh, preferred_element_type=jnp.float32)
            * scaling
        )
        .astype(jnp.bfloat16)
        .reshape(column_shape)
    )
    d_key = (
        (
            jnp.einsum("cnhtu,ctnhd->cunhd", d_scores, qh, preferred_element_type=jnp.float32)
            * scaling
        )
        .astype(jnp.bfloat16)
        .reshape(column_shape)
    )
    d_value = (
        jnp.einsum("cnhtu,ctnhd->cunhd", prob_half, dh, preferred_element_type=jnp.float32)
        .astype(jnp.bfloat16)
        .reshape(column_shape)
    )
    d_inputs_t = (
        project_back(d_query, w_query) + project_back(d_key, w_key) + project_back(d_value, w_value)
    ).astype(jnp.bfloat16)
    d_inputs = lax.all_to_all(d_inputs_t, "frame", split_axis=1, concat_axis=2, tiled=True)
    qkv_terms = [cross(latents_t, d_query), cross(latents_t, d_key), cross(latents_t, d_value)]
    grad_rows = (
        upstream.astype(jnp.float32) + d_inputs.reshape(-1, channels).astype(jnp.float32)
    ).astype(jnp.bfloat16)
    grad_input = grad_rows.reshape(clip_latents.shape)
    token_count = (
        clip_count
        * lax.axis_size("dp")
        * frame_count
        * lax.axis_size("frame")
        * pixels
        * lax.axis_size("height")
    )
    grad_scale = float(token_count) ** (-0.5)
    attn_term = jnp.concatenate(qkv_terms + [cross(mixed_rows, upstream)], axis=0) * grad_scale
    grad_attn = lax.psum_scatter(
        attn_term, ("frame", "height", "dp"), scatter_dimension=0, tiled=True
    )
    conv_term = jnp.concatenate(conv_terms, axis=0) * grad_scale
    summed = lax.psum(conv_term.astype(jnp.bfloat16), "frame")
    grad_conv = lax.psum_scatter(summed, ("height", "dp"), scatter_dimension=0, tiled=True).astype(
        jnp.float32
    )
    return (grad_input, grad_attn, grad_conv)


def solution(mesh):
    in_specs = (
        P("dp", "frame", "height", None, None),
        P("dp", "frame", "height", None, None),
        P("dp", "frame", "height", None),
        P(),
        P(),
        P(),
    )
    out_specs = (
        P("dp", "frame", "height", None, None),
        P(("frame", "height", "dp"), None),
        P(("height", "dp"), None),
    )
    return jax.shard_map(body, mesh=mesh, in_specs=in_specs, out_specs=out_specs, check_vma=False)
```

profile of v0, /device:TPU:0, one launch (start us, length us, event | category | flops | bytes accessed | tf_op | source)
XLA Modules:
  0.0 359.6 jit_solution(10459075539410474658)
XLA Ops:
  8.8 6.3 %all-to-all-start.1 = ((bf16[1,2,256]{1,0,2:T(2,128)(2,1)}), bf16[1,2,256]{1,0,2:T(2,128)(2,1)S(1)}, u32[]{:S(2)}, u32[]{:S(2)}) async-start(bf16[1,2,256]{1,0,2:T(2,128)(2,1)} %copy.236), calls=%async_computation.1 | async-start | bytes 262144 | tf_op jit(solution)/shard_map/all_to_all | solution.py:64
  15.2 2.1 copy.224
  17.3 3.9 %all-to-all-done.1 = bf16[1,2,256]{1,0,2:T(2,128)(2,1)S(1)} async-done(((bf16[1,2,256]{1,0,2:T(2,128)(2,1)}), bf16[1,2,256]{1,0,2:T(2,128)(2,1)S(1)}, u32[]{:S(2)}, u32[]{:S(2)}) %all-to-all-start.1) | async-done | bytes 1056 | tf_op jit(solution)/shard_map/all_to_all | solution.py:64
  21.3 3.5 all-to-all-start
  25.1 10.0 %all-to-all-done = bf16[1,2,256,320]{3,1,0,2:T(2,128)(2,1)S(1)} async-done(((bf16[1,2,256,320]{3,1,0,2:T(2,128)(2,1)}), bf16[1,2,256,320]{3,1,0,2:T(2,128)(2,1)S(1)}, u32[]{:S(2)}, u32[]{:S(2)}) %all-to-all-start) | async-done | bytes 327712 | tf_op jit(solution)/shard_map/all_to_all | solution.py:63
  37.6 1.2 copy.233
  39.1 1.2 copy.240
  40.4 3.3 fusion.59
  44.4 2.7 fusion.7
  47.2 1.6 copy.242
  48.8 1.0 copy.243
  49.8 3.6 all-to-all-start.2
  53.4 1.0 copy.246
  54.4 0.9 copy.223
  56.6 6.7 %all-to-all-done.2 = bf16[1,8,64,320]{3,2,0,1:T(8,128)(2,1)S(1)} async-done(((bf16[1,8,64,320]{3,2,0,1:T(8,128)(2,1)}), bf16[1,8,64,320]{3,2,0,1:T(8,128)(2,1)S(1)}, u32[]{:S(2)}, u32[]{:S(2)}) %all-to-all-start.2) | async-done | bytes 327712 | tf_op jit(solution)/shard_map/all_to_all | solution.py:86
  63.3 2.5 multiply_convert_fusion.2
  66.1 1.4 collective-permute-start.1
  67.6 4.7 %collective-permute-start = (bf16[1,2,1,16,640]{4,3,2,1,0:T(8,128)(2,1)S(1)}, bf16[1,2,1,16,640]{4,3,2,1,0:T(8,128)(2,1)S(1)}, u32[]{:S(2)}, u32[]{:S(2)}) collective-permute-start(bf16[1,2,1,16,640]{4,3,2,1,0:T(8,128)(2,1)S(1)} %get-tuple-element.29), channel_id=1, source_target_pairs={{0,2},{2,4},{4,6},{1,3},{3,5},{5,7},{8,10},{10,12},{12,14},{9,11},... | collective-permute-start | bytes 122888 | tf_op jit(solution)/shard_map/ppermute | solution.py:14
  72.8 1.0 collective-permute-done
  75.4 1.2 convolution_bitcast_fusion.8
  77.1 1.2 convolution_bitcast_fusion.7
  78.2 1.2 convolution_bitcast_fusion.6
  79.4 1.2 convolution_bitcast_fusion.5
  80.6 1.2 convolution_bitcast_fusion.3
  81.8 1.2 convolution_bitcast_fusion.2
  83.2 1.2 convolution_bitcast_fusion.1
  84.4 1.2 convolution_bitcast_fusion
  90.3 1.2 convolution_convert_fusion.5
  91.5 1.8 reshape.304
  93.3 2.0 copy.249
  95.3 4.1 %all-to-all-start.3 = ((bf16[1,2,256,320]{3,1,0,2:T(2,128)(2,1)}), bf16[1,2,256,320]{3,1,0,2:T(2,128)(2,1)}, u32[]{:S(2)}, u32[]{:S(2)}) async-start(bf16[1,2,256,320]{3,1,0,2:T(2,128)(2,1)} %copy.249), calls=%async_computation.3 | async-start | bytes 786432 | tf_op jit(solution)/shard_map/all_to_all | solution.py:129
  99.5 4.8 %concatenate.29 = f32[2880,320]{0,1:T(8,128)} concatenate(f32[320,320]{0,1:T(8,128)S(1)} %copy-done.5, f32[320,320]{0,1:T(8,128)} %convolution_bitcast_fusion.7, f32[320,320]{0,1:T(8,128)} %convolution_bitcast_fusion.6, f32[320,320]{0,1:T(8,128)} %convolution_bitcast_fusion.5, f32[320,320]{0,1:T(8,128)S(1)} %convolution_bitcast_fusion.4, f32[320,320]{0,1:T(8,128)} %convolution_bitcast_fusion.3, ...), dimensions={0} | concatenate | bytes 7372800 | tf_op jit(solution)/shard_map/concatenate | solution.py:178
  104.3 3.6 multiply_convert_fusion
  108.9 1.1 fusion.60
  110.0 1.0 copy.250
  111.4 1.2 copy.252
  112.5 2.6 multiply_reduce_fusion
  118.2 1.4 copy.268
  119.6 2.2 reshape_reshape.12
  121.8 1.4 copy.270
  123.2 2.2 reshape_reshape.13
  125.4 2.1 convolution_bitcast_fusion.11
  127.5 1.1 convolution_bitcast_fusion.10
  128.7 1.4 copy.271
  130.0 2.2 reshape_reshape.14
  132.3 2.1 convolution_bitcast_fusion.9
  134.4 1.3 copy.256
  135.7 1.3 copy.259
  137.0 1.3 copy.262
  138.3 1.9 concatenate.28
  140.2 2.5 fusion.34
  142.7 1.3 broadcast_multiply_fusion
  143.9 27.7 %all-reduce.11.cloned.1.call-done = bf16[2880,320]{0,1:T(8,128)(2,1)} async-done(((bf16[2880,320]{0,1:T(8,128)(2,1)}), bf16[2880,320]{0,1:T(8,128)(2,1)}) %all-reduce.11.cloned.1.call-update) | async-done | bytes 1843216
  171.6 1.8 constant_dynamic-slice_fusion
  173.5 1.9 convolution_add_fusion.1
  175.4 1.1 copy-done.2
  176.5 1.2 fusion.17
  177.7 4.9 %all-to-all-start.4 = ((bf16[1,8,64,320]{3,2,0,1:T(8,128)(2,1)}), bf16[1,8,64,320]{3,2,0,1:T(8,128)(2,1)S(1)}, u32[]{:S(2)}, u32[]{:S(2)}) async-start(bf16[1,8,64,320]{3,2,0,1:T(8,128)(2,1)} %fusion.17), calls=%async_computation.4 | async-start | bytes 786432 | tf_op jit(solution)/shard_map/all_to_all | solution.py:159
  182.6 13.3 %all-to-all-done.4 = bf16[1,8,64,320]{3,2,0,1:T(8,128)(2,1)S(1)} async-done(((bf16[1,8,64,320]{3,2,0,1:T(8,128)(2,1)}), bf16[1,8,64,320]{3,2,0,1:T(8,128)(2,1)S(1)}, u32[]{:S(2)}, u32[]{:S(2)}) %all-to-all-start.4) | async-done | bytes 327712 | tf_op jit(solution)/shard_map/all_to_all | solution.py:159
  196.3 0.9 copy.267
  197.2 16.2 %all-reduce.7.cloned.1.call-done = bf16[360,320]{0,1:T(8,128)(2,1)} async-done(((bf16[360,320]{0,1:T(8,128)(2,1)}), bf16[360,320]{0,1:T(8,128)(2,1)}) %all-reduce.7.cloned.1.call-update) | async-done | bytes 230416 | tf_op jit(solution)/shard_map/psum | solution.py:179
  213.4 1.8 convert_element_type.189
  215.1 136.1 %all-reduce.9.cloned.1.call-done = f32[1280,320]{0,1:T(8,128)} async-done(((f32[1280,320]{0,1:T(8,128)}), f32[1280,320]{0,1:T(8,128)}) %all-reduce.9.cloned.1.call-update) | async-done | bytes 1638416
  351.3 1.1 constant_dynamic-slice_fusion.1
  (92 shorter events, 19.3 us)
Async XLA Ops:
  7.2 17.6 %copy-start.17 = (f32[5,8,8]{2,1,0:T(8,128)S(1)}, f32[5,8,8]{2,1,0:T(8,128)}, u32[]{:S(2)}) copy-start(f32[5,8,8]{2,1,0:T(8,128)} %param.11) | copy-start | bytes 3844
  8.8 12.4 %all-to-all-start.1 = ((bf16[1,2,256]{1,0,2:T(2,128)(2,1)}), bf16[1,2,256]{1,0,2:T(2,128)(2,1)S(1)}, u32[]{:S(2)}, u32[]{:S(2)}) async-start(bf16[1,2,256]{1,0,2:T(2,128)(2,1)} %copy.236), calls=%async_computation.1 | async-start | bytes 262144 | tf_op jit(solution)/shard_map/all_to_all | solution.py:64
  17.3 17.9 %copy-start.1 = (bf16[1280,320]{0,1:T(8,128)(2,1)S(1)}, bf16[1280,320]{0,1:T(8,128)(2,1)}, u32[]{:S(2)}) copy-start(bf16[1280,320]{0,1:T(8,128)(2,1)} %param.9) | copy-start | bytes 2457604
  21.3 13.9 %all-to-all-start = ((bf16[1,2,256,320]{3,1,0,2:T(2,128)(2,1)}), bf16[1,2,256,320]{3,1,0,2:T(2,128)(2,1)S(1)}, u32[]{:S(2)}, u32[]{:S(2)}) async-start(bf16[1,2,256,320]{3,1,0,2:T(2,128)(2,1)} %bitcast.2), calls=%async_computation | async-start | bytes 786432 | tf_op jit(solution)/shard_map/all_to_all | solution.py:63
  40.4 4.0 %copy-start.11 = (bf16[8,64,5,64]{3,0,2,1:T(8,128)(2,1)S(1)}, bf16[8,64,5,64]{3,0,2,1:T(8,128)(2,1)}, u32[]{:S(2)}) copy-start(bf16[8,64,5,64]{3,0,2,1:T(8,128)(2,1)} %copy.240) | copy-start | bytes 983044
  43.7 0.7 copy-start.15
  47.2 6.2 %copy-start.6 = (bf16[1,2,16,16,320]{4,3,2,1,0:T(8,128)(2,1)S(1)}, bf16[1,2,16,16,320]{4,3,2,1,0:T(8,128)(2,1)}, u32[]{:S(2)}) copy-start(bf16[1,2,16,16,320]{4,3,2,1,0:T(8,128)(2,1)} %param.6) | copy-start | bytes 983044
  48.8 5.7 %copy-start = (bf16[1,2,16,16,320]{4,3,2,1,0:T(8,128)(2,1)S(1)}, bf16[1,2,16,16,320]{4,3,2,1,0:T(8,128)(2,1)}, u32[]{:S(2)}) copy-start(bf16[1,2,16,16,320]{4,3,2,1,0:T(8,128)(2,1)} %param.7) | copy-start | bytes 983044
  49.8 5.6 %copy-start.18 = (u32[32]{0:T(128)S(1)}, u32[32]{0:T(128)}, u32[]{:S(2)}) copy-start(u32[32]{0:T(128)} %constant.30) | copy-start | bytes 388
  49.8 13.5 %all-to-all-start.2 = ((bf16[1,8,64,320]{3,2,0,1:T(8,128)(2,1)}), bf16[1,8,64,320]{3,2,0,1:T(8,128)(2,1)S(1)}, u32[]{:S(2)}, u32[]{:S(2)}) async-start(bf16[1,8,64,320]{3,2,0,1:T(8,128)(2,1)} %copy.243), calls=%async_computation.2 | async-start | bytes 786432 | tf_op jit(solution)/shard_map/all_to_all | solution.py:86
  63.3 2.5 copy-start.7
  66.0 6.7 %copy-start.12 = (f32[2,256,320]{1,2,0:T(8,128)S(1)}, f32[2,256,320]{1,2,0:T(8,128)}, u32[]{:S(2)}) copy-start(f32[2,256,320]{1,2,0:T(8,128)} %get-tuple-element.34) | copy-start | bytes 1966084
  66.1 6.6 %collective-permute-start.1 = (bf16[1,2,1,16,640]{4,3,2,1,0:T(8,128)(2,1)S(1)}, bf16[1,2,1,16,640]{4,3,2,1,0:T(8,128)(2,1)S(1)}, u32[]{:S(2)}, u32[]{:S(2)}) collective-permute-start(bf16[1,2,1,16,640]{4,3,2,1,0:T(8,128)(2,1)S(1)} %get-tuple-element.30), channel_id=1, source_target_pairs={{2,0},{4,2},{6,4},{3,1},{5,3},{7,5},{10,8},{12,10},{14,12},{11,9},... | collective-permute-start | bytes 122888 | tf_op jit(solution)/shard_map/ppermute | solution.py:17
  67.6 6.2 %collective-permute-start = (bf16[1,2,1,16,640]{4,3,2,1,0:T(8,128)(2,1)S(1)}, bf16[1,2,1,16,640]{4,3,2,1,0:T(8,128)(2,1)S(1)}, u32[]{:S(2)}, u32[]{:S(2)}) collective-permute-start(bf16[1,2,1,16,640]{4,3,2,1,0:T(8,128)(2,1)S(1)} %get-tuple-element.29), channel_id=1, source_target_pairs={{0,2},{2,4},{4,6},{1,3},{3,5},{5,7},{8,10},{10,12},{12,14},{9,11},... | collective-permute-start | bytes 122888 | tf_op jit(solution)/shard_map/ppermute | solution.py:14
  83.2 2.4 copy-start.4
  88.7 1.0 copy-start.14
  90.2 9.2 %copy-start.5 = (f32[320,320]{0,1:T(8,128)S(1)}, f32[320,320]{0,1:T(8,128)}, u32[]{:S(2)}) copy-start(f32[320,320]{0,1:T(8,128)} %convolution_bitcast_fusion.8) | copy-start | bytes 1228804
  95.3 14.7 %all-to-all-start.3 = ((bf16[1,2,256,320]{3,1,0,2:T(2,128)(2,1)}), bf16[1,2,256,320]{3,1,0,2:T(2,128)(2,1)}, u32[]{:S(2)}, u32[]{:S(2)}) async-start(bf16[1,2,256,320]{3,1,0,2:T(2,128)(2,1)} %copy.249), calls=%async_computation.3 | async-start | bytes 786432 | tf_op jit(solution)/shard_map/all_to_all | solution.py:129
  99.4 72.2 %all-reduce.11.cloned.1.call-start = ((), (), s32[]{:S(2)}) async-start(), calls=%async_computation.7 | async-start | bytes 3768320
  107.9 1.0 copy-start.8
  107.9 105.5 %all-reduce.7.cloned.1.call-start = ((), (), s32[]{:S(2)}) async-start(), calls=%async_computation.5 | async-start | bytes 491520 | tf_op jit(solution)/shard_map/psum | solution.py:179
  112.5 2.6 copy-start.9
  112.5 2.6 copy-start.16
  115.5 1.1 copy-start.3
  116.6 1.1 copy-start.13
  125.4 2.1 copy-start.10
  173.4 177.9 %all-reduce.9.cloned.1.call-start = ((), (), s32[]{:S(2)}) async-start(), calls=%async_computation.6 | async-start | bytes 3276800
  175.4 1.1 copy-start.2
  177.7 18.2 %all-to-all-start.4 = ((bf16[1,8,64,320]{3,2,0,1:T(8,128)(2,1)}), bf16[1,8,64,320]{3,2,0,1:T(8,128)(2,1)S(1)}, u32[]{:S(2)}, u32[]{:S(2)}) async-start(bf16[1,8,64,320]{3,2,0,1:T(8,128)(2,1)} %fusion.17), calls=%async_computation.4 | async-start | bytes 786432 | tf_op jit(solution)/shard_map/all_to_all | solution.py:159
Sparse Core Ops, SparseCore 0:
  108.0 63.5 all-reduce.10
  174.5 38.8 all-reduce.6
  218.8 132.4 all-reduce.8
where the time goes:
time: 361 us; the launch traced here: 360 us
  waiting for transfers between devices  215 us (60%)
  local copies, waits for them, and re-layouts  50.6 us (14%)
  matrix products  41.3 us (11%)
  starting transfers between devices  28.9 us (8%)
  between operations  14.9 us (4%)
  other arithmetic  8.95 us (2%)
    unnamed x5, waiting for transfers between devices  164 us
    dot_general x13, matrix products, cross(): lax.dot_general(left_rows, right_rows, (((0,), (0,)), ((), ())), preferre...  16.4 us
    psum x1, waiting for transfers between devices, body(): summed = lax.psum(conv_term.astype(jnp.bfloat16), 'frame')  16.2 us
    all_to_all x1, waiting for transfers between devices, body(): lax.all_to_all(d_inputs_t, 'frame', split_axis=1, concat_axis=2, tiled=True)  13.3 us
    dot_general x13, matrix products, project_back(): lax.dot_general(flat_rows, weight, (((1,), (1,)), ((), ())), preferred_el...  10.9 us
    unnamed x44, local copies, waits for them, and re-layouts  10.5 us
    all_to_all x1, waiting for transfers between devices, body(): lax.all_to_all(flat_x, 'frame', split_axis=2, concat_axis=1, tiled=True)  10 us
  transfers between devices with their start and end apart: 10, of which 8 were waited for; matrix products, arithmetic and copies ran while one was open for 15% of the time, Pallas kernels for 0%

commit v1 on v0

--- a/solution.py
+++ b/solution.py
@@ -156,7 +156,9 @@
     d_inputs_t = (
         project_back(d_query, w_query) + project_back(d_key, w_key) + project_back(d_value, w_value)
     ).astype(jnp.bfloat16)
-    d_inputs = lax.all_to_all(d_inputs_t, "frame", split_axis=1, concat_axis=2, tiled=True)
+    pieces = jnp.split(d_inputs_t, lax.axis_size("frame"), axis=1)
+    received = lax.all_to_all(jnp.stack(pieces), "frame", 0, 0)
+    d_inputs = jnp.concatenate(received, axis=2)
     qkv_terms = [cross(latents_t, d_query), cross(latents_t, d_key), cross(latents_t, d_value)]
     grad_rows = (
         upstream.astype(jnp.float32) + d_inputs.reshape(-1, channels).astype(jnp.float32)

time: 361 us -> 354 us (0.981)
  local copies, waits for them, and re-layouts: 50.6 us -> 41.8 us
  waiting for transfers between devices: 215 us -> 222 us
  matrix products: 41.3 us -> 35.2 us
    psum x1, waiting for transfers between devices: 16.2 us -> 31.4 us  [body(): summed = lax.psum(conv_term.astype(jnp.bfloat16), 'frame')]
    all_to_all x1, waiting for transfers between devices: 13.3 us -> 0.01 us  [body(): received = lax.all_to_all(jnp.stack(pieces), 'frame', 0, 0)]
    another operation x3, local copies, waits for them, and re-layouts: 6.68 us -> 1.12 us  [project_back(): flat_rows = matrix.reshape(-1, matrix.shape[-1])]
    unnamed x5, waiting for transfers between devices: 164 us -> 169 us
    dot_general x13, matrix products: 16.4 us -> 12.7 us  [cross(): lax.dot_general(left_rows, right_rows, (((0,), (0,)), ((), ())), preferre...]
    unnamed x44 -> x50, local copies, waits for them, and re-layouts: 10.5 us -> 9.67 us
  transfers between devices with their start and end apart: 10 -> 10, of which waited for: 8 -> 7; matrix products, arithmetic and copies ran while one was open for 15% -> 13% of each run, Pallas kernels for 0% -> 0%
where the time goes in v1:
time: 354 us; the launch traced here: 353 us
  waiting for transfers between devices  222 us (63%)
  local copies, waits for them, and re-layouts  41.8 us (12%)
  matrix products  35.2 us (10%)
  starting transfers between devices  28.1 us (8%)
  between operations  15 us (4%)
  other arithmetic  10.8 us (3%)
    unnamed x5, waiting for transfers between devices  169 us
    psum x1, waiting for transfers between devices, body(): summed = lax.psum(conv_term.astype(jnp.bfloat16), 'frame')  31.4 us
    dot_general x13, matrix products, cross(): lax.dot_general(left_rows, right_rows, (((0,), (0,)), ((), ())), preferre...  12.7 us
    all_to_all x1, waiting for transfers between devices, body(): lax.all_to_all(flat_x, 'frame', split_axis=2, concat_axis=1, tiled=True)  10 us
    unnamed x50, local copies, waits for them, and re-layouts  9.67 us
    dot_general x13, matrix products, project_back(): lax.dot_general(flat_rows, weight, (((1,), (1,)), ((), ())), preferred_el...  8.4 us
  transfers between devices with their start and end apart: 10, of which 7 were waited for; matrix products, arithmetic and copies ran while one was open for 13% of the time, Pallas kernels for 0%

profile of v1, /device:TPU:0, one launch (start us, length us, event | category | flops | bytes accessed | tf_op | source)
XLA Modules:
  0.0 352.9 jit_solution(10346924453671182730)
XLA Ops:
  7.2 0.7 convert_element_type.153
  8.0 0.8 copy.234
  8.8 6.3 %all-to-all-start.1 = ((bf16[1,2,256]{1,0,2:T(2,128)(2,1)}), bf16[1,2,256]{1,0,2:T(2,128)(2,1)S(1)}, u32[]{:S(2)}, u32[]{:S(2)}) async-start(bf16[1,2,256]{1,0,2:T(2,128)(2,1)} %copy.234), calls=%async_computation.1 | async-start | bytes 262144 | tf_op jit(solution)/shard_map/all_to_all | solution.py:64
  15.2 2.1 copy.222
  17.3 3.9 %all-to-all-done.1 = bf16[1,2,256]{1,0,2:T(2,128)(2,1)S(1)} async-done(((bf16[1,2,256]{1,0,2:T(2,128)(2,1)}), bf16[1,2,256]{1,0,2:T(2,128)(2,1)S(1)}, u32[]{:S(2)}, u32[]{:S(2)}) %all-to-all-start.1) | async-done | bytes 1056 | tf_op jit(solution)/shard_map/all_to_all | solution.py:64
  21.3 3.5 all-to-all-start
  25.1 10.0 %all-to-all-done = bf16[1,2,256,320]{3,1,0,2:T(2,128)(2,1)S(1)} async-done(((bf16[1,2,256,320]{3,1,0,2:T(2,128)(2,1)}), bf16[1,2,256,320]{3,1,0,2:T(2,128)(2,1)S(1)}, u32[]{:S(2)}, u32[]{:S(2)}) %all-to-all-start) | async-done | bytes 327712 | tf_op jit(solution)/shard_map/all_to_all | solution.py:63
  36.2 1.2 convolution_convert_fusion.4
  38.8 1.6 copy.226
  40.3 1.2 copy.238
  41.5 2.2 fusion.59
  43.7 0.7 copy-done.18
  44.4 2.7 fusion.7
  47.1 1.6 copy.240
  48.7 1.0 copy.241
  49.7 3.6 %all-to-all-start.2 = ((bf16[1,8,64,320]{3,2,0,1:T(8,128)(2,1)}), bf16[1,8,64,320]{3,2,0,1:T(8,128)(2,1)S(1)}, u32[]{:S(2)}, u32[]{:S(2)}) async-start(bf16[1,8,64,320]{3,2,0,1:T(8,128)(2,1)} %copy.241), calls=%async_computation.2 | async-start | bytes 786432 | tf_op jit(solution)/shard_map/all_to_all | solution.py:86
  53.4 1.0 copy.244
  54.4 0.9 copy.221
  56.5 6.7 %all-to-all-done.2 = bf16[1,8,64,320]{3,2,0,1:T(8,128)(2,1)S(1)} async-done(((bf16[1,8,64,320]{3,2,0,1:T(8,128)(2,1)}), bf16[1,8,64,320]{3,2,0,1:T(8,128)(2,1)S(1)}, u32[]{:S(2)}, u32[]{:S(2)}) %all-to-all-start.2) | async-done | bytes 327712 | tf_op jit(solution)/shard_map/all_to_all | solution.py:86
  63.3 2.3 multiply_convert_fusion.2
  65.9 1.4 collective-permute-start.1
  67.3 4.7 %collective-permute-start = (bf16[1,2,1,16,640]{4,3,2,1,0:T(8,128)(2,1)S(1)}, bf16[1,2,1,16,640]{4,3,2,1,0:T(8,128)(2,1)S(1)}, u32[]{:S(2)}, u32[]{:S(2)}) collective-permute-start(bf16[1,2,1,16,640]{4,3,2,1,0:T(8,128)(2,1)S(1)} %get-tuple-element.29), channel_id=1, source_target_pairs={{0,2},{2,4},{4,6},{1,3},{3,5},{5,7},{8,10},{10,12},{12,14},{9,11},... | collective-permute-start | bytes 122888 | tf_op jit(solution)/shard_map/ppermute | solution.py:14
  72.6 1.0 collective-permute-done
  73.6 0.8 select_maximum_fusion
  74.4 0.8 fusion.58
  75.2 1.2 convolution_bitcast_fusion.8
  76.9 1.2 convolution_bitcast_fusion.7
  78.0 1.2 convolution_bitcast_fusion.6
  79.2 1.2 convolution_bitcast_fusion.5
  80.4 1.2 convolution_bitcast_fusion.3
  81.6 1.2 convolution_bitcast_fusion.2
  83.0 1.2 convolution_bitcast_fusion.1
  84.2 1.2 convolution_bitcast_fusion
  90.5 0.8 reshape.301
  91.3 2.0 copy.247
  93.3 3.5 all-to-all-start.3
  97.1 4.9 %concatenate.29 = f32[2880,320]{0,1:T(8,128)} concatenate(f32[320,320]{0,1:T(8,128)} %convolution_bitcast_fusion.8, f32[320,320]{0,1:T(8,128)} %convolution_bitcast_fusion.7, f32[320,320]{0,1:T(8,128)} %convolution_bitcast_fusion.6, f32[320,320]{0,1:T(8,128)} %convolution_bitcast_fusion.5, f32[320,320]{0,1:T(8,128)S(1)} %convolution_bitcast_fusion.4, ...), dimensions={0} | concatenate | bytes 7372800 | tf_op jit(solution)/shard_map/concatenate | solution.py:180
  102.0 3.6 %multiply_convert_fusion = bf16[2880,320]{0,1:T(8,128)(2,1)} fusion(f32[2880,320]{0,1:T(8,128)} %concatenate.29), kind=kLoop, calls=%fused_computation.1 | loop fusion | flops 1843200 | bytes 5529600 | tf_op jit(solution)/shard_map/convert_element_type | solution.py:181
  105.6 1.1 fusion.60
  107.1 1.2 copy.250
  108.4 2.4 multiply_reduce_fusion
  112.6 0.6 copy-done.15
  113.2 1.4 fusion.8
  114.6 1.3 copy.254
  115.9 1.6 fusion.34
  117.4 1.3 copy.257
  118.7 2.4 copy.260
  121.1 1.7 convolution_add_fusion.1
  123.3 0.7 slice_bitcast_fusion.19
  126.1 0.8 pad_maximum_fusion.1
  126.9 4.8 %all-to-all-start.4 = ((bf16[4,1,2,64,320]{4,3,2,1,0:T(8,128)(2,1)}), bf16[4,1,2,64,320]{4,3,2,1,0:T(8,128)(2,1)}, u32[]{:S(2)}, u32[]{:S(2)}) async-start(bf16[4,1,2,64,320]{4,3,2,1,0:T(8,128)(2,1)} %pad_maximum_fusion.1), calls=%async_computation.4 | async-start | bytes 786432 | tf_op jit(solution)/shard_map/all_to_all | solution.py:160
  133.5 1.1 convolution_bitcast_fusion.9
  134.7 1.5 concatenate.28
  136.2 32.9 %all-reduce.11.cloned.1.call-done = bf16[2880,320]{0,1:T(8,128)(2,1)} async-done(((bf16[2880,320]{0,1:T(8,128)(2,1)}), bf16[2880,320]{0,1:T(8,128)(2,1)}) %all-reduce.11.cloned.1.call-update) | async-done | bytes 1843216
  169.1 1.8 constant_dynamic-slice_fusion
  170.9 1.3 broadcast_multiply_fusion
  172.2 1.1 convert_bitcast_fusion
  173.6 0.6 copy-done.3
  174.4 0.9 copy.264
  175.3 31.4 %all-reduce.7.cloned.1.call-done = bf16[360,320]{0,1:T(8,128)(2,1)} async-done(((bf16[360,320]{0,1:T(8,128)(2,1)}), bf16[360,320]{0,1:T(8,128)(2,1)}) %all-reduce.7.cloned.1.call-update) | async-done | bytes 230416 | tf_op jit(solution)/shard_map/psum | solution.py:181
  206.7 1.8 convert_element_type.185
  208.5 136.1 %all-reduce.9.cloned.1.call-done = f32[1280,320]{0,1:T(8,128)} async-done(((f32[1280,320]{0,1:T(8,128)}), f32[1280,320]{0,1:T(8,128)}) %all-reduce.9.cloned.1.call-update) | async-done | bytes 1638416
  344.6 1.1 constant_dynamic-slice_fusion.1
  345.7 0.7 copy.271
  (101 shorter events, 17.4 us)
Async XLA Ops:
  7.2 17.6 %copy-start.20 = (f32[5,8,8]{2,1,0:T(8,128)S(1)}, f32[5,8,8]{2,1,0:T(8,128)}, u32[]{:S(2)}) copy-start(f32[5,8,8]{2,1,0:T(8,128)} %param.11) | copy-start | bytes 3844
  8.8 12.4 %all-to-all-start.1 = ((bf16[1,2,256]{1,0,2:T(2,128)(2,1)}), bf16[1,2,256]{1,0,2:T(2,128)(2,1)S(1)}, u32[]{:S(2)}, u32[]{:S(2)}) async-start(bf16[1,2,256]{1,0,2:T(2,128)(2,1)} %copy.234), calls=%async_computation.1 | async-start | bytes 262144 | tf_op jit(solution)/shard_map/all_to_all | solution.py:64
  17.3 17.9 %copy-start.1 = (bf16[1280,320]{0,1:T(8,128)(2,1)S(1)}, bf16[1280,320]{0,1:T(8,128)(2,1)}, u32[]{:S(2)}) copy-start(bf16[1280,320]{0,1:T(8,128)(2,1)} %param.9) | copy-start | bytes 2457604
  21.3 13.9 %all-to-all-start = ((bf16[1,2,256,320]{3,1,0,2:T(2,128)(2,1)}), bf16[1,2,256,320]{3,1,0,2:T(2,128)(2,1)S(1)}, u32[]{:S(2)}, u32[]{:S(2)}) async-start(bf16[1,2,256,320]{3,1,0,2:T(2,128)(2,1)} %bitcast.2), calls=%async_computation | async-start | bytes 786432 | tf_op jit(solution)/shard_map/all_to_all | solution.py:63
  38.8 4.9 %copy-start.6 = (bf16[8,64,5,64]{3,0,2,1:T(8,128)(2,1)}, bf16[8,64,5,64]{3,0,2,1:T(8,128)(2,1)S(1)}, u32[]{:S(2)}) copy-start(bf16[8,64,5,64]{3,0,2,1:T(8,128)(2,1)S(1)} %copy.231) | copy-start | bytes 983044
  41.5 2.9 copy-start.12
  43.7 0.7 copy-start.18
  47.1 6.2 %copy-start.10 = (bf16[1,2,16,16,320]{4,3,2,1,0:T(8,128)(2,1)S(1)}, bf16[1,2,16,16,320]{4,3,2,1,0:T(8,128)(2,1)}, u32[]{:S(2)}) copy-start(bf16[1,2,16,16,320]{4,3,2,1,0:T(8,128)(2,1)} %param.6) | copy-start | bytes 983044
  48.7 5.7 %copy-start = (bf16[1,2,16,16,320]{4,3,2,1,0:T(8,128)(2,1)S(1)}, bf16[1,2,16,16,320]{4,3,2,1,0:T(8,128)(2,1)}, u32[]{:S(2)}) copy-start(bf16[1,2,16,16,320]{4,3,2,1,0:T(8,128)(2,1)} %param.7) | copy-start | bytes 983044
  49.7 5.6 %copy-start.21 = (u32[32]{0:T(128)S(1)}, u32[32]{0:T(128)}, u32[]{:S(2)}) copy-start(u32[32]{0:T(128)} %constant.30) | copy-start | bytes 388
  49.7 13.5 %all-to-all-start.2 = ((bf16[1,8,64,320]{3,2,0,1:T(8,128)(2,1)}), bf16[1,8,64,320]{3,2,0,1:T(8,128)(2,1)S(1)}, u32[]{:S(2)}, u32[]{:S(2)}) async-start(bf16[1,8,64,320]{3,2,0,1:T(8,128)(2,1)} %copy.241), calls=%async_computation.2 | async-start | bytes 786432 | tf_op jit(solution)/shard_map/all_to_all | solution.py:86
  65.8 6.7 %copy-start.14 = (f32[2,256,320]{1,2,0:T(8,128)S(1)}, f32[2,256,320]{1,2,0:T(8,128)}, u32[]{:S(2)}) copy-start(f32[2,256,320]{1,2,0:T(8,128)} %get-tuple-element.38) | copy-start | bytes 1966084
  65.9 6.6 %collective-permute-start.1 = (bf16[1,2,1,16,640]{4,3,2,1,0:T(8,128)(2,1)S(1)}, bf16[1,2,1,16,640]{4,3,2,1,0:T(8,128)(2,1)S(1)}, u32[]{:S(2)}, u32[]{:S(2)}) collective-permute-start(bf16[1,2,1,16,640]{4,3,2,1,0:T(8,128)(2,1)S(1)} %get-tuple-element.30), channel_id=1, source_target_pairs={{2,0},{4,2},{6,4},{3,1},{5,3},{7,5},{10,8},{12,10},{14,12},{11,9},... | collective-permute-start | bytes 122888 | tf_op jit(solution)/shard_map/ppermute | solution.py:17
  67.3 6.2 %collective-permute-start = (bf16[1,2,1,16,640]{4,3,2,1,0:T(8,128)(2,1)S(1)}, bf16[1,2,1,16,640]{4,3,2,1,0:T(8,128)(2,1)S(1)}, u32[]{:S(2)}, u32[]{:S(2)}) collective-permute-start(bf16[1,2,1,16,640]{4,3,2,1,0:T(8,128)(2,1)S(1)} %get-tuple-element.29), channel_id=1, source_target_pairs={{0,2},{2,4},{4,6},{1,3},{3,5},{5,7},{8,10},{10,12},{12,14},{9,11},... | collective-permute-start | bytes 122888 | tf_op jit(solution)/shard_map/ppermute | solution.py:14
  83.0 2.4 copy-start.8
  88.5 1.0 copy-start.17
  90.0 15.6 %copy-start.2 = (bf16[512,320]{0,1:T(8,128)(2,1)}, bf16[512,320]{0,1:T(8,128)(2,1)S(1)}, u32[]{:S(2)}) copy-start(bf16[512,320]{0,1:T(8,128)(2,1)S(1)} %fusion.15) | copy-start | bytes 983044
  93.3 13.4 %all-to-all-start.3 = ((bf16[1,2,256,320]{3,1,0,2:T(2,128)(2,1)}), bf16[1,2,256,320]{3,1,0,2:T(2,128)(2,1)S(1)}, u32[]{:S(2)}, u32[]{:S(2)}) async-start(bf16[1,2,256,320]{3,1,0,2:T(2,128)(2,1)} %copy.247), calls=%async_computation.3 | async-start | bytes 786432 | tf_op jit(solution)/shard_map/all_to_all | solution.py:129
  96.8 72.3 %all-reduce.11.cloned.1.call-start = ((), (), s32[]{:S(2)}) async-start(), calls=%async_computation.7 | async-start | bytes 3768320
  106.7 1.6 copy-start.19
  107.1 1.3 copy-start.13
  108.4 2.4 copy-start.11
  111.0 1.1 copy-start.7
  112.1 1.1 copy-start.15
  121.1 1.7 copy-start.5
  124.0 1.2 copy-start.4
  125.2 0.9 copy-start.16
  126.9 45.3 %all-to-all-start.4 = ((bf16[4,1,2,64,320]{4,3,2,1,0:T(8,128)(2,1)}), bf16[4,1,2,64,320]{4,3,2,1,0:T(8,128)(2,1)}, u32[]{:S(2)}, u32[]{:S(2)}) async-start(bf16[4,1,2,64,320]{4,3,2,1,0:T(8,128)(2,1)} %pad_maximum_fusion.1), calls=%async_computation.4 | async-start | bytes 786432 | tf_op jit(solution)/shard_map/all_to_all | solution.py:160
  131.7 75.0 %all-reduce.7.cloned.1.call-start = ((), (), s32[]{:S(2)}) async-start(), calls=%async_computation.5 | async-start | bytes 491520 | tf_op jit(solution)/shard_map/psum | solution.py:181
  133.2 1.5 copy-start.9
  170.9 173.7 %all-reduce.9.cloned.1.call-start = ((), (), s32[]{:S(2)}) async-start(), calls=%async_computation.6 | async-start | bytes 3276800
  173.3 1.0 copy-start.3
Sparse Core Ops, SparseCore 0:
  105.7 63.3 all-reduce.10
  172.0 34.7 all-reduce.6
  212.1 132.4 all-reduce.8
